TPU v7x, 32 devices: a whole 2x2x4 slice. The times are simulated.
32 devices in a mesh: seq: 16 (over z, y, x), tp: 2 (over core).
Axes of the slice: x: 2, y: 2, z: 4, core: 2. Of those that a mesh axis runs over, the one named last changes fastest.
Arguments:
- img_qkv: bfloat16 [1, 512, 3, 2048], P(None, 'seq', None, 'tp'), may hold values from -7 to 7
- txt_qkv: bfloat16 [1, 256, 3, 2048], P(None, None, None, 'tp'), may hold values from -7 to 7
- frame_index: int32 [1, 512], P(None, 'seq'), may hold values from 0 to 32
- row_index: int32 [1, 512], P(None, 'seq'), may hold values from 0 to 44
- column_index: int32 [1, 512], P(None, 'seq'), may hold values from 0 to 79
- txt_len: int32 [1], replicated, may hold values from 64 to 256
- residual: bfloat16 [1, 512, 3072], P(None, ('seq', 'tp')), may hold values from -6 to 6
- w_proj: bfloat16 [2048, 3072], P('tp'), may hold values from -0.125 to 0.125
- proj_bias: float32 [3072], replicated, may hold values from -3 to 3
- gate: float32 [3072], replicated, may hold values from -4 to 4
Outputs:
- img_out: bfloat16 [1, 512, 3072], P(None, ('seq', 'tp'))
- txt_out: bfloat16 [1, 256, 2048], P(None, None, 'tp')
All inputs are finite; a program needn't handle non-finite values.
Results may differ from a plain program's by a relative error of at most 0.0082.
Values may be sent and summed in bfloat16 or wider, within the bound.
A program may use at most 64 MiB of HBM per device.

v0:
```python
import math

import jax
import jax.numpy as jnp
from jax import lax
from jax.sharding import PartitionSpec as P

HD = 128


rope_base = 256.0
neg_large = -1e30


def rope_tables(frame_index, row_index, column_index, head_dim):
    frame_part = head_dim // 8
    second = (head_dim - frame_part) // 2
    pieces = []
    for places, part_width in (
        (frame_index, frame_part),
        (row_index, second),
        (column_index, second),
    ):
        pair_ids = jnp.arange(part_width // 2).astype(jnp.float32)
        pair_rates = rope_base ** (-2.0 * pair_ids / part_width)
        pieces.append(places.astype(jnp.float32)[:, None] * pair_rates[None, :])
    angles = jnp.repeat(jnp.concatenate(pieces, axis=1), 2, axis=1)
    parity = jnp.arange(head_dim) % 2
    signed = jnp.where(parity == 0, -1.0, 1.0).astype(jnp.float32)
    return (jnp.cos(angles), jnp.sin(angles) * signed[None, :])


def rotate(block_in, cosine, sine_table):
    values = block_in.astype(jnp.float32)
    parity = jnp.arange(values.shape[-1]) % 2
    partner = jnp.where(parity == 0, jnp.roll(values, -1, axis=-1), jnp.roll(values, 1, axis=-1))
    return (values * cosine[:, None, :] + partner * sine_table[:, None, :]).astype(jnp.bfloat16)


def absorb(carry_state, queries, block_keys, block_values, live_keys, score_scale):
    peak, weight_sum, blended = carry_state
    scores = (
        jnp.einsum("cqd,ckd->cqk", queries, block_keys, preferred_element_type=jnp.float32)
        * score_scale
    )
    if live_keys is not None:
        scores = jnp.where(live_keys[:, None, :], scores, neg_large)
    new_peak = jnp.maximum(peak, jnp.max(scores, axis=2))
    weights = jnp.exp(scores - new_peak[:, :, None])
    if live_keys is not None:
        weights = jnp.where(live_keys[:, None, :], weights, 0.0)
    shrink = jnp.exp(peak - new_peak)
    weight_sum = weight_sum * shrink + jnp.sum(weights, axis=2)
    blended = blended * shrink[:, :, None] + jnp.einsum(
        "cqk,ckd->cqd",
        weights.astype(jnp.bfloat16),
        block_values,
        preferred_element_type=jnp.float32,
    )
    return (new_peak, weight_sum, blended)


def shards(
    img_qkv,
    txt_qkv,
    frame_index,
    row_index,
    column_index,
    txt_len,
    residual,
    w_proj,
    proj_bias,
    gate,
):
    clips = img_qkv.shape[0]
    clip_tok = img_qkv.shape[1]
    head_dim = HD
    heads_tp = img_qkv.shape[3] // head_dim
    seq_count = lax.axis_size("seq")
    tp_count = lax.axis_size("tp")
    groups = seq_count // heads_tp
    per_group = clip_tok // groups
    txt_total = txt_qkv.shape[1]
    txt_share = txt_total // groups
    position = lax.axis_index("seq")
    my_head = position % heads_tp
    my_group = position // heads_tp
    score_scale = 1.0 / math.sqrt(head_dim)
    cosine, sine_table = rope_tables(
        frame_index.reshape(-1), row_index.reshape(-1), column_index.reshape(-1), head_dim
    )
    img_query = rotate(
        img_qkv[:, :, 0].reshape(clips * clip_tok, heads_tp, head_dim), cosine, sine_table
    ).reshape(clips, clip_tok, heads_tp, head_dim)
    img_key = rotate(
        img_qkv[:, :, 1].reshape(clips * clip_tok, heads_tp, head_dim), cosine, sine_table
    ).reshape(clips, clip_tok, heads_tp, head_dim)
    img_value = img_qkv[:, :, 2].reshape(clips, clip_tok, heads_tp, head_dim)
    query_send = (
        img_query.reshape(clips, groups, per_group, heads_tp, head_dim)
        .transpose(1, 3, 0, 2, 4)
        .reshape(seq_count, clips * per_group, head_dim)
    )
    key_value = jnp.stack([img_key, img_value], axis=2)
    txt_head = lax.dynamic_slice_in_dim(txt_qkv, my_head * head_dim, head_dim, 3)
    txt_query = lax.dynamic_slice_in_dim(txt_head[:, :, 0], my_group * txt_share, txt_share, 1)
    img_rows_count = seq_count * per_group
    query_rows = img_rows_count + txt_share
    start_state = (
        jnp.full((clips, query_rows), neg_large, jnp.float32),
        jnp.zeros((clips, query_rows), jnp.float32),
        jnp.zeros((clips, query_rows, head_dim), jnp.float32),
    )
    copies = jnp.broadcast_to(
        key_value.transpose(3, 0, 1, 2, 4)[None], (groups, heads_tp, clips, clip_tok, 2, head_dim)
    ).reshape(seq_count, clips, clip_tok, 2, head_dim)
    query_recv, pair_recv = (
        lax.all_to_all(query_send, "seq", split_axis=0, concat_axis=0, tiled=True),
        lax.all_to_all(copies, "seq", split_axis=0, concat_axis=0, tiled=True),
    )
    ordered = (
        query_recv.reshape(seq_count, clips, per_group, head_dim)
        .transpose(1, 0, 2, 3)
        .reshape(clips, img_rows_count, head_dim)
    )
    queries = jnp.concatenate([ordered, txt_query], axis=1)
    sources = max(1, min(seq_count, 2048 // clip_tok))
    while seq_count % sources:
        sources -= 1
    all_pairs = pair_recv.transpose(1, 0, 2, 3, 4).reshape(
        clips, seq_count // sources, sources * clip_tok, 2, head_dim
    )
    key_blocks = all_pairs.transpose(1, 0, 2, 3, 4)

    def sweep_block(carry_state, key_block):
        return (
            absorb(carry_state, queries, key_block[:, :, 0], key_block[:, :, 1], None, score_scale),
            None,
        )

    carry_state, unused = lax.scan(sweep_block, start_state, key_blocks)
    txt_live = jnp.arange(txt_total)[None, :] < txt_len[:, None]
    peak, weight_sum, blended = absorb(
        carry_state, queries, txt_head[:, :, 1], txt_head[:, :, 2], txt_live, score_scale
    )
    attended = (blended / weight_sum[:, :, None]).astype(jnp.bfloat16)
    img_part = (
        attended[:, :img_rows_count]
        .reshape(clips, seq_count, per_group, head_dim)
        .transpose(1, 0, 2, 3)
    )
    txt_part = attended[:, img_rows_count:]
    returned = lax.all_to_all(img_part, "seq", split_axis=0, concat_axis=0, tiled=True)
    home_rows = (
        returned.reshape(groups, heads_tp, clips, per_group, head_dim)
        .transpose(2, 0, 3, 1, 4)
        .reshape(clips, clip_tok, heads_tp * head_dim)
    )
    txt_index = my_group * txt_share + jnp.arange(txt_share)
    txt_keep = (txt_index[None, :] < txt_len[:, None])[:, :, None]
    txt_part = jnp.where(txt_keep, txt_part, jnp.zeros_like(txt_part))
    gathered = lax.all_gather(txt_part[None], "seq", axis=0, tiled=True)
    txt_out = (
        gathered.reshape(groups, heads_tp, clips, txt_share, head_dim)
        .transpose(2, 0, 3, 1, 4)
        .reshape(clips, txt_total, heads_tp * head_dim)
    )
    row_share = clip_tok // tp_count
    share_rows = clips * row_share
    ordered_rows = (
        home_rows.reshape(clips, tp_count, row_share, heads_tp * head_dim)
        .transpose(1, 0, 2, 3)
        .reshape(tp_count * share_rows, heads_tp * head_dim)
    )
    projected = lax.psum_scatter(
        jnp.dot(ordered_rows, w_proj, preferred_element_type=jnp.float32).astype(jnp.bfloat16),
        "tp",
        scatter_dimension=0,
        tiled=True,
    ).astype(jnp.float32)
    projected = projected.reshape(clips, row_share, projected.shape[1])
    img_out = (
        residual.astype(jnp.float32) + gate[None, None, :] * (projected + proj_bias[None, None, :])
    ).astype(jnp.bfloat16)
    return (img_out, txt_out)


def solution(mesh):
    in_specs = (
        P(None, "seq", None, "tp"),
        P(None, None, None, "tp"),
        P(None, "seq"),
        P(None, "seq"),
        P(None, "seq"),
        P(),
        P(None, ("seq", "tp"), None),
        P("tp", None),
        P(),
        P(),
    )
    out_specs = (P(None, ("seq", "tp"), None), P(None, None, "tp"))
    return jax.shard_map(shards, mesh=mesh, in_specs=in_specs, out_specs=out_specs, check_vma=False)
```

profile of v0, /device:TPU:0, one launch (start us, length us, event | category | flops | bytes accessed | tf_op | source)
XLA Modules:
  0.0 106.6 jit_solution(7230840717838111667)
XLA Ops:
  7.3 1.0 convert_bitcast_fusion.1
  8.7 0.1 fusion.26
  8.9 0.1 sin.17
  9.1 0.2 broadcast_multiply_fusion
  9.4 0.1 cos.17
  9.6 0.2 fusion.24
  9.7 0.6 copy.53
  10.4 8.3 %all-to-all-start = ((bf16[16,16,128]{2,1,0:T(8,128)(2,1)}), bf16[16,16,128]{2,1,0:T(8,128)(2,1)S(1)}, u32[]{:S(2)}, u32[]{:S(2)}) async-start(bf16[16,16,128]{2,1,0:T(8,128)(2,1)} %bitcast.8), calls=%async_computation | async-start | bytes 131072 | tf_op jit(solution)/shard_map/all_to_all | solution.py:118
  19.0 0.1 broadcast_multiply_fusion.1
  19.2 0.1 copy.57
  19.3 0.1 copy.55
  19.5 0.2 copy.56
  19.6 0.1 copy.58
  19.8 0.1 fusion.21
  20.0 6.2 %all-to-all-done = bf16[16,16,128]{2,1,0:T(8,128)(2,1)S(1)} async-done(((bf16[16,16,128]{2,1,0:T(8,128)(2,1)}), bf16[16,16,128]{2,1,0:T(8,128)(2,1)S(1)}, u32[]{:S(2)}, u32[]{:S(2)}) %all-to-all-start) | async-done | bytes 65568 | tf_op jit(solution)/shard_map/all_to_all | solution.py:118
  26.3 0.8 broadcast_in_dim.105
  27.0 3.5 %all-to-all-start.1 = ((bf16[16,1,32,2,128]{4,2,3,1,0:T(8,128)(2,1)}), bf16[16,1,32,2,128]{4,2,3,1,0:T(8,128)(2,1)S(1)}, u32[]{:S(2)}, u32[]{:S(2)}) async-start(bf16[16,1,32,2,128]{4,2,3,1,0:T(8,128)(2,1)} %bitcast.21), calls=%async_computation.1 | async-start | bytes 524288 | tf_op jit(solution)/shard_map/all_to_all | solution.py:119
  31.3 0.2 fusion.38
  31.5 7.5 %all-to-all-done.1 = bf16[16,1,32,2,128]{4,2,3,1,0:T(8,128)(2,1)S(1)} async-done(((bf16[16,1,32,2,128]{4,2,3,1,0:T(8,128)(2,1)}), bf16[16,1,32,2,128]{4,2,3,1,0:T(8,128)(2,1)S(1)}, u32[]{:S(2)}, u32[]{:S(2)}) %all-to-all-start.1) | async-done | bytes 262176 | tf_op jit(solution)/shard_map/all_to_all | solution.py:119
  39.1 0.3 fusion.37
  39.4 0.1 fusion.9
  39.5 0.3 fusion.5
  39.8 0.3 fusion.2
  40.2 0.3 fusion.4
  40.5 0.6 slice.88
  41.2 3.7 %all-to-all-start.2 = ((bf16[16,1,16,128]{3,2,1,0:T(8,128)(2,1)}), bf16[16,1,16,128]{3,2,1,0:T(8,128)(2,1)S(1)}, u32[]{:S(2)}, u32[]{:S(2)}) async-start(bf16[16,1,16,128]{3,2,1,0:T(8,128)(2,1)} %bitcast.30), calls=%async_computation.2 | async-start | bytes 131072 | tf_op jit(solution)/shard_map/all_to_all | solution.py:153
  44.9 7.5 %all-to-all-done.2 = bf16[16,1,16,128]{3,2,1,0:T(8,128)(2,1)S(1)} async-done(((bf16[16,1,16,128]{3,2,1,0:T(8,128)(2,1)}), bf16[16,1,16,128]{3,2,1,0:T(8,128)(2,1)S(1)}, u32[]{:S(2)}, u32[]{:S(2)}) %all-to-all-start.2) | async-done | bytes 65568 | tf_op jit(solution)/shard_map/all_to_all | solution.py:153
  52.4 4.7 %convolution_convert_fusion = bf16[32,3072]{1,0:T(8,128)(2,1)} fusion(bf16[1024,3072]{1,0:T(8,128)(2,1)} %param.17, bf16[4,8,8,128]{3,2,1,0:T(8,128)(2,1)S(1)} %bitcast.138), kind=kOutput, calls=%fused_computation | convolution fusion | flops 201424896 | bytes 6553600 | tf_op jit(solution)/shard_map/dot_general | solution.py:176
  57.2 39.6 %all-gather = bf16[16,128,128]{2,1,0:T(8,128)(2,1)S(1)} all-gather(bf16[1,128,128]{2,1,0:T(8,128)(2,1)S(1)} %slice_select_fusion), channel_id=2, replica_groups=mesh['seq'=16,'tp'=2] {'seq'}, dimensions={0}, use_global_device_ids=true | all-gather | bytes 557056 | tf_op jit(solution)/shard_map/all_gather | solution.py:162
  96.8 0.3 copy.65
  97.1 1.0 reshape.419
  98.1 1.6 %fusion.12 = bf16[1,16,3072]{2,1,0:T(8,128)(2,1)} fusion(bf16[16,3072]{1,0:T(8,128)(2,1)} %reduce-scatter.2.cloned.1.call-done, bf16[1,16,3072]{2,1,0:T(8,128)(2,1)S(1)} %copy-done.1, f32[3072]{0:T(1024)S(1)} %copy-done.2, f32[3072]{0:T(1024)S(1)} %copy-done.3), kind=kLoop, calls=%fused_computation.18 | loop fusion | flops 294912 | bytes 319488 | tf_op jit(solution)/shard_map/convert_element_type | solution.py:184
  (48 shorter events, 1.2 us)
Async XLA Ops:
  7.2 24.1 %copy-start = (bf16[1,256,3,1024]{3,1,2,0:T(8,128)(2,1)S(1)}, bf16[1,256,3,1024]{3,1,2,0:T(8,128)(2,1)}, u32[]{:S(2)}) copy-start(bf16[1,256,3,1024]{3,1,2,0:T(8,128)(2,1)} %param.11) | copy-start | bytes 4718596
  7.2 1.4 %copy-start.6 = (s32[1,32]{1,0:T(1,128)S(1)}, s32[1,32]{1,0:T(1,128)}, u32[]{:S(2)}) copy-start(s32[1,32]{1,0:T(1,128)} %param.12) | copy-start | bytes 388
  7.2 1.4 %copy-start.4 = (s32[1,32]{1,0:T(1,128)S(1)}, s32[1,32]{1,0:T(1,128)}, u32[]{:S(2)}) copy-start(s32[1,32]{1,0:T(1,128)} %param.14) | copy-start | bytes 388
  7.2 1.4 %copy-start.5 = (s32[1,32]{1,0:T(1,128)S(1)}, s32[1,32]{1,0:T(1,128)}, u32[]{:S(2)}) copy-start(s32[1,32]{1,0:T(1,128)} %param.13) | copy-start | bytes 388
  10.4 15.9 %all-to-all-start = ((bf16[16,16,128]{2,1,0:T(8,128)(2,1)}), bf16[16,16,128]{2,1,0:T(8,128)(2,1)S(1)}, u32[]{:S(2)}, u32[]{:S(2)}) async-start(bf16[16,16,128]{2,1,0:T(8,128)(2,1)} %bitcast.8), calls=%async_computation | async-start | bytes 131072 | tf_op jit(solution)/shard_map/all_to_all | solution.py:118
  27.0 12.0 %all-to-all-start.1 = ((bf16[16,1,32,2,128]{4,2,3,1,0:T(8,128)(2,1)}), bf16[16,1,32,2,128]{4,2,3,1,0:T(8,128)(2,1)S(1)}, u32[]{:S(2)}, u32[]{:S(2)}) async-start(bf16[16,1,32,2,128]{4,2,3,1,0:T(8,128)(2,1)} %bitcast.21), calls=%async_computation.1 | async-start | bytes 524288 | tf_op jit(solution)/shard_map/all_to_all | solution.py:119
  41.2 11.2 %all-to-all-start.2 = ((bf16[16,1,16,128]{3,2,1,0:T(8,128)(2,1)}), bf16[16,1,16,128]{3,2,1,0:T(8,128)(2,1)S(1)}, u32[]{:S(2)}, u32[]{:S(2)}) async-start(bf16[16,1,16,128]{3,2,1,0:T(8,128)(2,1)} %bitcast.30), calls=%async_computation.2 | async-start | bytes 131072 | tf_op jit(solution)/shard_map/all_to_all | solution.py:153
  44.9 53.3 %reduce-scatter.2.cloned.1.call-start = ((), (), s32[]{:S(2)}) async-start(), calls=%async_computation.4 | async-start | bytes 294912 | tf_op jit(solution)/shard_map/reduce_scatter | solution.py:175
  57.1 41.0 %copy-start.1 = (bf16[1,16,3072]{2,1,0:T(8,128)(2,1)S(1)}, bf16[1,16,3072]{2,1,0:T(8,128)(2,1)}, u32[]{:S(2)}) copy-start(bf16[1,16,3072]{2,1,0:T(8,128)(2,1)} %param.16) | copy-start | bytes 294916
  57.1 41.0 %copy-start.2 = (f32[3072]{0:T(1024)S(1)}, f32[3072]{0:T(1024)}, u32[]{:S(2)}) copy-start(f32[3072]{0:T(1024)} %param.18) | copy-start | bytes 36868
  57.1 41.0 %copy-start.3 = (f32[3072]{0:T(1024)S(1)}, f32[3072]{0:T(1024)}, u32[]{:S(2)}) copy-start(f32[3072]{0:T(1024)} %param.19) | copy-start | bytes 36868
Sparse Core Ops, SparseCore 0:
  57.2 4.3 reduce-scatter.1
where the time goes:
time: 107 us
  blocking collectives  39.6 us (37%)
  waiting for transfers between devices  21.2 us (20%)
  starting transfers between devices  15.6 us (15%)
  between operations  15 us (14%)
  matrix products  5.93 us (6%)
  local copies, waits for them, and re-layouts  5.11 us (5%)
  other arithmetic  4.09 us (4%)
    all_gather x1, blocking collectives, shards(): gathered = lax.all_gather(txt_part[None], 'seq', axis=0, tiled=True)  39.6 us
    all_to_all x1, starting transfers between devices, shards(): lax.all_to_all(query_send, 'seq', split_axis=0, concat_axis=0, tiled=True)  8.34 us
    all_to_all x1, waiting for transfers between devices, shards(): lax.all_to_all(copies, 'seq', split_axis=0, concat_axis=0, tiled=True)  7.49 us
    all_to_all x1, waiting for transfers between devices, shards(): lax.all_to_all(img_part, 'seq', split_axis=0, concat_axis=0, tiled=True)  7.47 us
    all_to_all x1, waiting for transfers between devices, shards(): lax.all_to_all(query_send, 'seq', split_axis=0, concat_axis=0, tiled=True)  6.25 us
    dot_general x1, matrix products, shards(): jnp.dot(ordered_rows, w_proj, preferred_element_type=jnp.float32)  4.66 us
    all_to_all x1, starting transfers between devices, shards(): lax.all_to_all(img_part, 'seq', split_axis=0, concat_axis=0, tiled=True)  3.69 us
    all_to_all x1, starting transfers between devices, shards(): lax.all_to_all(copies, 'seq', split_axis=0, concat_axis=0, tiled=True)  3.53 us
  transfers between devices with their start and end apart: 4, of which 3 were waited for; matrix products, arithmetic and copies ran while one was open for 3% of the time, Pallas kernels for 0%

commit v1 on v0

v1 whole, which is shorter than its diff:
```python
import functools
import math

import jax
import jax.numpy as jnp
import numpy as np
from jax import lax
from jax.experimental import pallas as pl
from jax.experimental.pallas import tpu as pltpu
from jax.sharding import PartitionSpec as P

HD = 128
ROPE_BASE = 256.0
NEG_LARGE = -1e30
F32 = jnp.float32
BF16 = jnp.bfloat16


def pair_rates():
    first = HD // 8
    second = (HD - first) // 2
    rates = np.zeros((3, HD), np.float32)
    start = 0
    for part, width in enumerate((first, second, second)):
        ids = np.arange(width // 2, dtype=np.float64)
        rates[part, start : start + width] = np.repeat(ROPE_BASE ** (-2.0 * ids / width), 2)
        start += width
    return rates


def largest_divisor(n):
    best = 1
    for d in range(1, n + 1):
        if n % d == 0 and d * d <= n:
            best = d
    return best


def kernel(
    n, heads, img_ref, txt_ref, pos_ref, rates_ref, len_ref, res_hbm, w_hbm, bias_hbm, gate_hbm,
    out_ref, txt_out,
    q_send, k_send, q_all, k_all, v_all, a_send, home, t_send, w, res, bias, gate, p_send, p_recv,
    local_sem, q_ss, q_rs, k_ss, k_rs, v_ss, v_rs, a_ss, a_rs, t1_ss, t2_ss, t_rs, p_ss, p_rs,
):
    p = lax.axis_index("seq")
    t = lax.axis_index("tp")
    groups = n // heads
    head = p // groups
    group = p % groups
    tokens = img_ref.shape[1]
    text = txt_ref.shape[1]
    share = text // groups
    image_keys = n * tokens
    scale = 1.0 / math.sqrt(HD)
    chunks = p_send.shape[0]
    width = p_send.shape[2]
    half = tokens // 2
    plane = largest_divisor(n)
    lines = n // plane

    loads = [
        pltpu.make_async_copy(src, dst, local_sem.at[i])
        for i, (src, dst) in enumerate(
            ((w_hbm, w), (res_hbm, res), (bias_hbm, bias), (gate_hbm, gate))
        )
    ]
    for load in loads:
        load.start()

    barrier = pltpu.get_barrier_semaphore()

    def greet(o, carry):
        pl.semaphore_signal(barrier, inc=1, device_id={"seq": (p + o) % n})
        return carry

    lax.fori_loop(1, n, greet, 0)
    pl.semaphore_signal(barrier, inc=1, device_id={"tp": 1 - t})

    diagonal = lax.broadcasted_iota(jnp.int32, (tokens, tokens), 0) == lax.broadcasted_iota(
        jnp.int32, (tokens, tokens), 1
    )
    angles = jnp.zeros((tokens, HD), F32)
    for part in range(3):
        row = pos_ref[part : part + 1, :].astype(F32)
        column = jnp.sum(jnp.where(diagonal, row, 0.0), axis=1, keepdims=True)
        angles = angles + column * rates_ref[part : part + 1, :]
    even = lax.broadcasted_iota(jnp.int32, (tokens, HD), 1) % 2 == 0
    cosine = jnp.cos(angles)
    sine = jnp.where(even, -1.0, 1.0) * jnp.sin(angles)
    for which, dst in ((0, q_send), (1, k_send)):
        for h in range(heads):
            x = img_ref[which, :, h * HD : (h + 1) * HD].astype(F32)
            partner = jnp.where(even, pltpu.roll(x, HD - 1, 1), pltpu.roll(x, 1, 1))
            dst[h] = (x * cosine + partner * sine).astype(BF16)

    pl.semaphore_wait(barrier, n)

    def rows(s):
        return pl.ds(pl.multiple_of(s * tokens, tokens), tokens)

    def cols(h):
        return pl.ds(pl.multiple_of(h * HD, HD), HD)

    def q_copy(h, src_line):
        return pltpu.make_async_remote_copy(
            q_send.at[h], q_all.at[rows(src_line)], q_ss.at[h], q_rs.at[src_line],
            device_id={"seq": h * groups + group},
        )

    def k_copy(d, s):
        return pltpu.make_async_remote_copy(
            k_send.at[d // groups], k_all.at[rows(s)], k_ss.at[d], k_rs.at[s], device_id={"seq": d}
        )

    def v_copy(d, s):
        return pltpu.make_async_remote_copy(
            img_ref.at[2, :, cols(d // groups)], v_all.at[rows(s)], v_ss.at[d], v_rs.at[s],
            device_id={"seq": d},
        )

    def a_copy(j, h):
        return pltpu.make_async_remote_copy(
            a_send.at[rows(j)], home.at[:, cols(h)], a_ss.at[j], a_rs.at[h],
            device_id={"seq": j * groups + group},
        )

    def over(count, f):
        def step(o, carry):
            f(o)
            return carry

        lax.fori_loop(1, count, step, 0)

    over(n, lambda o: k_copy((p + o) % n, p).start())
    over(heads, lambda o: q_copy((head + o) % heads, head).start())
    over(n, lambda o: v_copy((p + o) % n, p).start())

    q_all[rows(head), :] = q_send[head]
    k_all[rows(p), :] = k_send[head]
    v_all[rows(p), :] = img_ref[2, :, cols(head)]
    k_all[image_keys : image_keys + text, :] = txt_ref[1]
    v_all[image_keys : image_keys + text, :] = txt_ref[2]
    length = len_ref[0]

    def weigh(queries):
        scores = lax.dot_general(
            queries, k_all[...], (((1,), (1,)), ((), ())), preferred_element_type=F32
        )
        live = lax.broadcasted_iota(jnp.int32, scores.shape, 1) < image_keys + length
        scores = jnp.where(live, scores, NEG_LARGE)
        peak = jnp.max(scores, axis=1, keepdims=True)
        weights = jnp.where(live, jnp.exp((scores - peak) * scale), 0.0)
        return weights.astype(BF16), jnp.sum(weights, axis=1, keepdims=True)

    def blend(weights, total):
        return jnp.dot(weights, v_all[...], preferred_element_type=F32) / total

    over(n, lambda o: k_copy((p + o) % n, (p + n - o) % n).wait_recv())
    text_weights, text_total = weigh(txt_ref[0, pl.ds(pl.multiple_of(group * share, share), share), :])
    over(n, lambda o: v_copy((p + o) % n, (p + n - o) % n).wait_recv())
    text_done = blend(text_weights, text_total)
    text_row = lax.broadcasted_iota(jnp.int32, text_done.shape, 0) + group * share
    text_done = jnp.where(text_row < length, text_done, 0.0).astype(BF16)

    def block(s):
        return txt_out.at[
            pl.ds(pl.multiple_of((s % groups) * share, share), share), cols(s // groups)
        ]

    def line_copy(o, s):
        return pltpu.make_async_remote_copy(
            t_send, block(s), t1_ss.at[o], t_rs.at[s], device_id={"seq": (p + o * plane) % n}
        )

    def plane_copy(i, o, s):
        source = t_send if i is None else block(s)
        slot = 0 if i is None else i
        return pltpu.make_async_remote_copy(
            source, block(s), t2_ss.at[slot, o], t_rs.at[s],
            device_id={"seq": (p // plane) * plane + (p % plane + o) % plane},
        )

    t_send[...] = text_done
    txt_out[pl.ds(pl.multiple_of(group * share, share), share), cols(head)] = text_done
    over(lines, lambda o: line_copy(o, p).start())
    over(plane, lambda o: plane_copy(None, o, p).start())

    over(heads, lambda o: q_copy((head + o) % heads, (head + heads - o) % heads).wait_recv())
    a_send[...] = blend(*weigh(q_all[...])).astype(BF16)
    over(heads, lambda o: a_copy((head + o) % heads, head).start())
    home[:, cols(head)] = a_send[rows(head), :]

    def forward(i):
        s = (p + n - i * plane) % n
        line_copy(i, s).wait_recv()
        over(plane, lambda o: plane_copy(i, o, s).start())

    over(lines, forward)

    over(heads, lambda o: a_copy((head + o) % heads, (head + heads - o) % heads).wait_recv())
    for load in loads:
        load.wait()

    def p_copy(c):
        return pltpu.make_async_remote_copy(
            p_send.at[c], p_recv.at[c], p_ss.at[c], p_rs.at[c], device_id={"tp": 1 - t}
        )

    mine = []
    for c in range(chunks):
        part = jnp.dot(home[...], w[:, c * width : (c + 1) * width], preferred_element_type=F32)
        top, bottom = part[:half], part[half:]
        p_send[c] = jnp.where(t == 0, bottom, top).astype(BF16)
        p_copy(c).start()
        at = slice(c * width, (c + 1) * width)
        mine.append(jnp.where(t == 0, top, bottom))
    for c in range(chunks):
        at = slice(c * width, (c + 1) * width)
        p_copy(c).wait_recv()
        projected = mine[c] + p_recv[c].astype(F32)
        out_ref[:, at] = (
            res[:, at].astype(F32) + gate[:, at] * (projected + bias[:, at])
        ).astype(BF16)

    def finish_line(i):
        s = (p + n - i * plane) % n
        over(plane, lambda o: plane_copy(i, o, s).wait_send())
        line_copy(i, s).wait_send()

    def finish_plane(o):
        def one(i, carry):
            s = i * plane + (p % plane + o) % plane
            plane_copy(None, o, s).wait_recv()
            return carry

        lax.fori_loop(0, lines, one, 0)
        plane_copy(None, o, p).wait_send()

    over(plane, finish_plane)
    over(lines, finish_line)
    over(n, lambda o: k_copy((p + o) % n, p).wait_send())
    over(n, lambda o: v_copy((p + o) % n, p).wait_send())
    over(heads, lambda o: q_copy((head + o) % heads, head).wait_send())
    over(heads, lambda o: a_copy((head + o) % heads, head).wait_send())
    for c in range(chunks):
        p_copy(c).wait_send()


def shards(img_qkv, txt_qkv, frame_index, row_index, column_index, txt_len, residual, w_proj, proj_bias, gate):
    tokens = img_qkv.shape[1]
    channels = img_qkv.shape[3]
    heads = channels // HD
    n = lax.axis_size("seq")
    groups = n // heads
    text = txt_qkv.shape[1]
    share = text // groups
    plane = largest_divisor(n)
    lines = n // plane
    model = w_proj.shape[1]
    half = residual.shape[1]
    chunks = 4
    head = lax.axis_index("seq") // groups
    img = img_qkv[0].transpose(1, 0, 2)
    txt = lax.dynamic_slice_in_dim(txt_qkv[0], head * HD, HD, 2).transpose(1, 0, 2)
    positions = jnp.concatenate([frame_index, row_index, column_index], axis=0)
    vmem = pl.BlockSpec(memory_space=pltpu.VMEM)
    anyspace = pl.BlockSpec(memory_space=pl.ANY)
    dma = pltpu.SemaphoreType.DMA
    out, txt_out = pl.pallas_call(
        functools.partial(kernel, n, heads),
        out_shape=(
            jax.ShapeDtypeStruct((half, model), BF16),
            jax.ShapeDtypeStruct((text, channels), BF16),
        ),
        in_specs=[vmem, vmem, vmem, vmem, pl.BlockSpec(memory_space=pltpu.SMEM)] + [anyspace] * 4,
        out_specs=(vmem, vmem),
        scratch_shapes=[
            pltpu.VMEM((heads, tokens, HD), BF16),
            pltpu.VMEM((heads, tokens, HD), BF16),
            pltpu.VMEM((heads * tokens, HD), BF16),
            pltpu.VMEM((n * tokens + text, HD), BF16),
            pltpu.VMEM((n * tokens + text, HD), BF16),
            pltpu.VMEM((heads * tokens, HD), BF16),
            pltpu.VMEM((tokens, channels), BF16),
            pltpu.VMEM((share, HD), BF16),
            pltpu.VMEM(w_proj.shape, BF16),
            pltpu.VMEM((half, model), BF16),
            pltpu.VMEM((1, model), F32),
            pltpu.VMEM((1, model), F32),
            pltpu.VMEM((chunks, half, model // chunks), BF16),
            pltpu.VMEM((chunks, half, model // chunks), BF16),
            dma((4,)),
            dma((heads,)), dma((heads,)),
            dma((n,)), dma((n,)),
            dma((n,)), dma((n,)),
            dma((heads,)), dma((heads,)),
            dma((lines,)), dma((lines, plane)), dma((n,)),
            dma((chunks,)), dma((chunks,)),
        ],
        compiler_params=pltpu.CompilerParams(
            collective_id=0, has_side_effects=True, vmem_limit_bytes=48 * 1024 * 1024
        ),
    )(
        img, txt, positions, jnp.asarray(pair_rates()), txt_len, residual[0], w_proj,
        proj_bias[None], gate[None],
    )
    return out[None], txt_out[None]


def solution(mesh):
    in_specs = (
        P(None, "seq", None, "tp"),
        P(None, None, None, "tp"),
        P(None, "seq"),
        P(None, "seq"),
        P(None, "seq"),
        P(),
        P(None, ("seq", "tp"), None),
        P("tp", None),
        P(),
        P(),
    )
    out_specs = (P(None, ("seq", "tp"), None), P(None, None, "tp"))
    return jax.shard_map(shards, mesh=mesh, in_specs=in_specs, out_specs=out_specs, check_vma=False)
```

time: 107 us -> 35.1 us (0.33)
  blocking collectives: 39.6 us -> 0 us
  Pallas kernels: 0 us -> 27.2 us
  waiting for transfers between devices: 21.2 us -> 0 us
  starting transfers between devices: 15.6 us -> 0 us
  between operations: 15 us -> 1.45 us
  matrix products: 5.93 us -> 0 us
  other arithmetic: 4.09 us -> 0.7 us
    all_gather x1 -> x0, blocking collectives: 39.6 us -> none  [shards(): gathered = lax.all_gather(txt_part[None], 'seq', axis=0, tiled=True)]
    pallas_call x0 -> x1, Pallas kernels: none -> 27.2 us  [shards(): pl.pallas_call(functools.partial(kernel, n, heads), out_shape=(jax.ShapeD...]
    all_to_all x3 -> x0, waiting for transfers between devices: 21.2 us -> none  [the longest x1 7.49 us: shards(): lax.all_to_all(copies, 'seq', split_axis=0, concat_axis=0, tiled=True)]
    all_to_all x3 -> x0, starting transfers between devices: 15.6 us -> none  [the longest x1 8.34 us: shards(): lax.all_to_all(query_send, 'seq', split_axis=0, concat_axis=0, tiled=True)]
    dot_general x5 -> x0, matrix products: 5.93 us -> none  [the longest x1 4.66 us: shards(): jnp.dot(ordered_rows, w_proj, preferred_element_type=jnp.float32)]
    unnamed x17 -> x14, local copies, waits for them, and re-layouts: 0.1 us -> 5.35 us
    convert_element_type x4 -> x0, other arithmetic: 1.73 us -> none  [the longest x1 1.58 us: shards(): img_out = (residual.astype(jnp.float32) + gate[None, None, :] * (projecte...]
    slice x6 -> x0, local copies, waits for them, and re-layouts: 1.19 us -> none  [the longest x1 0.63 us: shards(): attended[:, :img_rows_count].reshape(clips, seq_count, per_group, head_dim)]
  transfers between devices with their start and end apart: 4 -> 0, of which waited for: 3 -> 0; matrix products, arithmetic and copies ran while one was open for 3% -> 0% of each run, Pallas kernels for 0% -> 0%
where the time goes in v1:
time: 35.1 us; the launch traced here: 34.7 us
  Pallas kernels  27.2 us (77%)
  local copies, waits for them, and re-layouts  5.41 us (15%)
  between operations  1.45 us (4%)
  other arithmetic  0.7 us (2%)
    pallas_call x1, Pallas kernels, shards(): pl.pallas_call(functools.partial(kernel, n, heads), out_shape=(jax.ShapeD...  27.2 us
    unnamed x14, local copies, waits for them, and re-layouts  5.35 us

profile of v1, /device:TPU:0, one launch (start us, length us, event | category | flops | bytes accessed | tf_op | source)
XLA Modules:
  0.0 34.7 jit_solution(2833080862801544895)
XLA Ops:
  0.6 0.0 copy-start
  1.4 0.7 %pad_add_fusion.pos_ref = s32[3,32]{1,0:T(4,128)S(1)} fusion(s32[1,32]{1,0:T(1,128)} %param.15, s32[1,32]{1,0:T(1,128)} %param.14, s32[1,32]{1,0:T(1,128)} %param.13), kind=kLoop, calls=%fused_computation.1 | loop fusion | flops 192 | bytes 768 | tf_op jit(solution)/shard_map/concatenate | solution.py:265
  2.1 0.0 copy-done
  2.1 0.1 dynamic-slice_bitcast_fusion.txt_ref
  2.2 0.0 copy-start.1
  2.2 0.9 %copy-done.1 = bf16[1,32,3,1024]{3,1,2,0:T(8,128)(2,1)S(1)} copy-done((bf16[1,32,3,1024]{3,1,2,0:T(8,128)(2,1)S(1)}, bf16[1,32,3,1024]{3,1,2,0:T(8,128)(2,1)}, u32[]{:S(2)}) %copy-start.1) | copy-done | bytes 196632
  3.1 0.0 copy-start.2
  3.1 0.9 %copy-done.2 = bf16[1,16,3072]{2,1,0:T(8,128)(2,1)S(1)} copy-done((bf16[1,16,3072]{2,1,0:T(8,128)(2,1)S(1)}, bf16[1,16,3072]{2,1,0:T(8,128)(2,1)}, u32[]{:S(2)}) %copy-start.2) | copy-done | bytes 98328
  4.0 0.0 copy-start.3
  4.0 0.7 %copy-done.3 = f32[3072]{0:T(1024)S(1)} copy-done((f32[3072]{0:T(1024)S(1)}, f32[3072]{0:T(1024)}, u32[]{:S(2)}) %copy-start.3) | copy-done | bytes 12312
  4.7 0.0 copy-start.4
  4.7 0.7 %copy-done.4 = f32[3072]{0:T(1024)S(1)} copy-done((f32[3072]{0:T(1024)S(1)}, f32[3072]{0:T(1024)}, u32[]{:S(2)}) %copy-start.4) | copy-done | bytes 12312
  5.4 0.0 copy-start.5
  5.4 0.7 %copy-done.5 = f32[3,128]{1,0:T(4,128)S(1)} copy-done((f32[3,128]{1,0:T(4,128)S(1)}, f32[3,128]{1,0:T(4,128)}, u32[]{:S(2)}) %copy-start.5) | copy-done | bytes 1560
  6.1 27.2 %shard_map.122 = (bf16[16,3072]{1,0:T(8,128)(2,1)S(1)}, bf16[256,1024]{1,0:T(8,128)(2,1)S(1)}) custom-call(bf16[3,32,1024]{2,1,0:T(8,128)(2,1)S(1)} %bitcast.13, bf16[3,256,128]{2,1,0:T(8,128)(2,1)S(1)} %dynamic-slice_bitcast_fusion.txt_ref, s32[3,32]{1,0:T(4,128)S(1)} %pad_add_fusion.pos_ref, f32[3,128]{1,0:T(4,128)S(1)} %copy-done.5, s32[1]{0:T(128)S(6)} %copy.15.len_ref, ...), custom_call_target="tpu_custom_call" | custom-call | tf_op jit(solution)/shard_map/pallas_call | solution.py:269
  33.3 0.6 %copy.16 = bf16[1,16,3072]{2,1,0:T(8,128)(2,1)} copy(bf16[1,16,3072]{2,1,0:T(8,128)(2,1)S(1)} %bitcast.14) | data formatting | bytes 196608
  33.9 0.8 %copy.17 = bf16[1,256,1024]{2,1,0:T(8,128)(2,1)} copy(bf16[1,256,1024]{2,1,0:T(8,128)(2,1)S(1)} %bitcast.12) | data formatting | bytes 1048576
Async XLA Ops:
  0.6 1.5 %copy-start = (bf16[1,256,3,1024]{3,1,2,0:T(8,128)(2,1)S(1)}, bf16[1,256,3,1024]{3,1,2,0:T(8,128)(2,1)}, u32[]{:S(2)}) copy-start(bf16[1,256,3,1024]{3,1,2,0:T(8,128)(2,1)} %param.12) | copy-start | bytes 4718596
  2.2 0.9 %copy-start.1 = (bf16[1,32,3,1024]{3,1,2,0:T(8,128)(2,1)S(1)}, bf16[1,32,3,1024]{3,1,2,0:T(8,128)(2,1)}, u32[]{:S(2)}) copy-start(bf16[1,32,3,1024]{3,1,2,0:T(8,128)(2,1)} %param.11) | copy-start | bytes 589828
  3.1 0.9 %copy-start.2 = (bf16[1,16,3072]{2,1,0:T(8,128)(2,1)S(1)}, bf16[1,16,3072]{2,1,0:T(8,128)(2,1)}, u32[]{:S(2)}) copy-start(bf16[1,16,3072]{2,1,0:T(8,128)(2,1)} %param.17) | copy-start | bytes 294916
  4.0 0.7 %copy-start.3 = (f32[3072]{0:T(1024)S(1)}, f32[3072]{0:T(1024)}, u32[]{:S(2)}) copy-start(f32[3072]{0:T(1024)} %param.19) | copy-start | bytes 36868
  4.7 0.7 %copy-start.4 = (f32[3072]{0:T(1024)S(1)}, f32[3072]{0:T(1024)}, u32[]{:S(2)}) copy-start(f32[3072]{0:T(1024)} %param.20) | copy-start | bytes 36868
  5.4 0.7 %copy-start.5 = (f32[3,128]{1,0:T(4,128)S(1)}, f32[3,128]{1,0:T(4,128)}, u32[]{:S(2)}) copy-start(f32[3,128]{1,0:T(4,128)} %constant.28.clone.rates_ref) | copy-start | bytes 4612

commit v2 on v1

--- a/solution.py
+++ b/solution.py
@@ -3,29 +3,16 @@
 
 import jax
 import jax.numpy as jnp
-import numpy as np
 from jax import lax
 from jax.experimental import pallas as pl
 from jax.experimental.pallas import tpu as pltpu
 from jax.sharding import PartitionSpec as P
 
 HD = 128
-ROPE_BASE = 256.0
+ROPE_BASE_LOG2 = 8.0
 NEG_LARGE = -1e30
 F32 = jnp.float32
 BF16 = jnp.bfloat16
-
-
-def pair_rates():
-    first = HD // 8
-    second = (HD - first) // 2
-    rates = np.zeros((3, HD), np.float32)
-    start = 0
-    for part, width in enumerate((first, second, second)):
-        ids = np.arange(width // 2, dtype=np.float64)
-        rates[part, start : start + width] = np.repeat(ROPE_BASE ** (-2.0 * ids / width), 2)
-        start += width
-    return rates
 
 
 def largest_divisor(n):
@@ -37,9 +24,9 @@
 
 
 def kernel(
-    n, heads, img_ref, txt_ref, pos_ref, rates_ref, len_ref, res_hbm, w_hbm, bias_hbm, gate_hbm,
+    n, heads, img_hbm, txt_hbm, frame_hbm, row_hbm, column_hbm, len_ref, res_hbm, w_hbm, bias_hbm, gate_hbm,
     out_ref, txt_out,
-    q_send, k_send, q_all, k_all, v_all, a_send, home, t_send, w, res, bias, gate, p_send, p_recv,
+    img_ref, txt_q, places, q_send, k_send, q_all, k_all, v_all, a_send, home, t_send, w, res, bias, gate, p_send, p_recv,
     local_sem, q_ss, q_rs, k_ss, k_rs, v_ss, v_rs, a_ss, a_rs, t1_ss, t2_ss, t_rs, p_ss, p_rs,
 ):
     p = lax.axis_index("seq")
@@ -48,7 +35,7 @@
     head = p // groups
     group = p % groups
     tokens = img_ref.shape[1]
-    text = txt_ref.shape[1]
+    text = txt_hbm.shape[1]
     share = text // groups
     image_keys = n * tokens
     scale = 1.0 / math.sqrt(HD)
@@ -58,13 +45,38 @@
     plane = largest_divisor(n)
     lines = n // plane
 
-    loads = [
-        pltpu.make_async_copy(src, dst, local_sem.at[i])
-        for i, (src, dst) in enumerate(
-            ((w_hbm, w), (res_hbm, res), (bias_hbm, bias), (gate_hbm, gate))
-        )
-    ]
-    for load in loads:
+    def rows(s):
+        return pl.ds(pl.multiple_of(s * tokens, tokens), tokens)
+
+    def cols(h):
+        return pl.ds(pl.multiple_of(h * HD, HD), HD)
+
+    text_rows = pl.ds(pl.multiple_of(group * share, share), share)
+    text_keys = pl.ds(image_keys, text)
+    early, middle, late = (
+        [pltpu.make_async_copy(src, dst, local_sem.at[first + i]) for i, (src, dst) in enumerate(pairs)]
+        for first, pairs in (
+            (
+                0,
+                (
+                    (frame_hbm, places.at[0]),
+                    (row_hbm, places.at[1]),
+                    (column_hbm, places.at[2]),
+                    (img_hbm, img_ref),
+                ),
+            ),
+            (
+                4,
+                (
+                    (txt_hbm.at[0, text_rows, cols(head)], txt_q),
+                    (txt_hbm.at[1, :, cols(head)], k_all.at[text_keys]),
+                    (txt_hbm.at[2, :, cols(head)], v_all.at[text_keys]),
+                ),
+            ),
+            (7, ((w_hbm, w), (res_hbm, res), (bias_hbm, bias), (gate_hbm, gate))),
+        )
+    )
+    for load in early + middle + late:
         load.start()
 
     barrier = pltpu.get_barrier_semaphore()
@@ -79,11 +91,22 @@
     diagonal = lax.broadcasted_iota(jnp.int32, (tokens, tokens), 0) == lax.broadcasted_iota(
         jnp.int32, (tokens, tokens), 1
     )
+    channel = lax.broadcasted_iota(jnp.int32, (1, HD), 1)
+    first = HD // 8
+    second = (HD - first) // 2
     angles = jnp.zeros((tokens, HD), F32)
-    for part in range(3):
-        row = pos_ref[part : part + 1, :].astype(F32)
-        column = jnp.sum(jnp.where(diagonal, row, 0.0), axis=1, keepdims=True)
-        angles = angles + column * rates_ref[part : part + 1, :]
+    for load in early:
+        load.wait()
+    for part, (start, size) in enumerate(
+        ((0, first), (first, second), (first + second, second))
+    ):
+        inside = (channel >= start) & (channel < start + size)
+        pair = ((channel - start) // 2).astype(F32)
+        rate = jnp.where(inside, jnp.exp2(pair * (-2.0 * ROPE_BASE_LOG2 / size)), 0.0)
+        column = jnp.sum(
+            jnp.where(diagonal, places[part].astype(F32), 0.0), axis=1, keepdims=True
+        )
+        angles = angles + column * rate
     even = lax.broadcasted_iota(jnp.int32, (tokens, HD), 1) % 2 == 0
     cosine = jnp.cos(angles)
     sine = jnp.where(even, -1.0, 1.0) * jnp.sin(angles)
@@ -95,12 +118,6 @@
 
     pl.semaphore_wait(barrier, n)
 
-    def rows(s):
-        return pl.ds(pl.multiple_of(s * tokens, tokens), tokens)
-
-    def cols(h):
-        return pl.ds(pl.multiple_of(h * HD, HD), HD)
-
     def q_copy(h, src_line):
         return pltpu.make_async_remote_copy(
             q_send.at[h], q_all.at[rows(src_line)], q_ss.at[h], q_rs.at[src_line],
@@ -138,8 +155,8 @@
     q_all[rows(head), :] = q_send[head]
     k_all[rows(p), :] = k_send[head]
     v_all[rows(p), :] = img_ref[2, :, cols(head)]
-    k_all[image_keys : image_keys + text, :] = txt_ref[1]
-    v_all[image_keys : image_keys + text, :] = txt_ref[2]
+    for load in middle:
+        load.wait()
     length = len_ref[0]
 
     def weigh(queries):
@@ -156,7 +173,9 @@
         return jnp.dot(weights, v_all[...], preferred_element_type=F32) / total
 
     over(n, lambda o: k_copy((p + o) % n, (p + n - o) % n).wait_recv())
-    text_weights, text_total = weigh(txt_ref[0, pl.ds(pl.multiple_of(group * share, share), share), :])
+    text_weights, text_total = weigh(txt_q[...])
+    over(heads, lambda o: q_copy((head + o) % heads, (head + heads - o) % heads).wait_recv())
+    image_weights, image_total = weigh(q_all[...])
     over(n, lambda o: v_copy((p + o) % n, (p + n - o) % n).wait_recv())
     text_done = blend(text_weights, text_total)
     text_row = lax.broadcasted_iota(jnp.int32, text_done.shape, 0) + group * share
@@ -185,8 +204,7 @@
     over(lines, lambda o: line_copy(o, p).start())
     over(plane, lambda o: plane_copy(None, o, p).start())
 
-    over(heads, lambda o: q_copy((head + o) % heads, (head + heads - o) % heads).wait_recv())
-    a_send[...] = blend(*weigh(q_all[...])).astype(BF16)
+    a_send[...] = blend(image_weights, image_total).astype(BF16)
     over(heads, lambda o: a_copy((head + o) % heads, head).start())
     home[:, cols(head)] = a_send[rows(head), :]
 
@@ -198,7 +216,7 @@
     over(lines, forward)
 
     over(heads, lambda o: a_copy((head + o) % heads, (head + heads - o) % heads).wait_recv())
-    for load in loads:
+    for load in late:
         load.wait()
 
     def p_copy(c):
@@ -246,6 +264,17 @@
         p_copy(c).wait_send()
 
 
+def store(img_ref, txt_ref, img_hbm, txt_hbm, sem):
+    copies = [
+        pltpu.make_async_copy(txt_ref, txt_hbm.at[0], sem.at[0]),
+        pltpu.make_async_copy(img_ref, img_hbm.at[0], sem.at[1]),
+    ]
+    for copy in copies:
+        copy.start()
+    for copy in copies:
+        copy.wait()
+
+
 def shards(img_qkv, txt_qkv, frame_index, row_index, column_index, txt_len, residual, w_proj, proj_bias, gate):
     tokens = img_qkv.shape[1]
     channels = img_qkv.shape[3]
@@ -259,12 +288,10 @@
     model = w_proj.shape[1]
     half = residual.shape[1]
     chunks = 4
-    head = lax.axis_index("seq") // groups
     img = img_qkv[0].transpose(1, 0, 2)
-    txt = lax.dynamic_slice_in_dim(txt_qkv[0], head * HD, HD, 2).transpose(1, 0, 2)
-    positions = jnp.concatenate([frame_index, row_index, column_index], axis=0)
+    txt = txt_qkv[0].transpose(1, 0, 2)
     vmem = pl.BlockSpec(memory_space=pltpu.VMEM)
-    anyspace = pl.BlockSpec(memory_space=pl.ANY)
+    hbm = pl.BlockSpec(memory_space=pltpu.HBM)
     dma = pltpu.SemaphoreType.DMA
     out, txt_out = pl.pallas_call(
         functools.partial(kernel, n, heads),
@@ -272,9 +299,12 @@
             jax.ShapeDtypeStruct((half, model), BF16),
             jax.ShapeDtypeStruct((text, channels), BF16),
         ),
-        in_specs=[vmem, vmem, vmem, vmem, pl.BlockSpec(memory_space=pltpu.SMEM)] + [anyspace] * 4,
+        in_specs=[hbm] * 5 + [pl.BlockSpec(memory_space=pltpu.SMEM)] + [hbm] * 4,
         out_specs=(vmem, vmem),
         scratch_shapes=[
+            pltpu.VMEM((3, tokens, channels), BF16),
+            pltpu.VMEM((share, HD), BF16),
+            pltpu.VMEM((3, 1, tokens), jnp.int32),
             pltpu.VMEM((heads, tokens, HD), BF16),
             pltpu.VMEM((heads, tokens, HD), BF16),
             pltpu.VMEM((heads * tokens, HD), BF16),
@@ -289,7 +319,7 @@
             pltpu.VMEM((1, model), F32),
             pltpu.VMEM((chunks, half, model // chunks), BF16),
             pltpu.VMEM((chunks, half, model // chunks), BF16),
-            dma((4,)),
+            dma((11,)),
             dma((heads,)), dma((heads,)),
             dma((n,)), dma((n,)),
             dma((n,)), dma((n,)),
@@ -298,13 +328,23 @@
             dma((chunks,)), dma((chunks,)),
         ],
         compiler_params=pltpu.CompilerParams(
-            collective_id=0, has_side_effects=True, vmem_limit_bytes=48 * 1024 * 1024
+            collective_id=0, has_side_effects=True, vmem_limit_bytes=67043328
         ),
     )(
-        img, txt, positions, jnp.asarray(pair_rates()), txt_len, residual[0], w_proj,
+        img, txt, frame_index, row_index, column_index, txt_len, residual[0], w_proj,
         proj_bias[None], gate[None],
     )
-    return out[None], txt_out[None]
+    return pl.pallas_call(
+        store,
+        out_shape=(
+            jax.ShapeDtypeStruct((1,) + out.shape, BF16),
+            jax.ShapeDtypeStruct((1,) + txt_out.shape, BF16),
+        ),
+        in_specs=[vmem, vmem],
+        out_specs=(hbm, hbm),
+        scratch_shapes=[dma((2,))],
+        compiler_params=pltpu.CompilerParams(vmem_limit_bytes=66400000),
+    )(out, txt_out)
 
 
 def solution(mesh):

time: 35.1 us -> 31.4 us (0.89)
  local copies, waits for them, and re-layouts: 5.41 us -> 0 us
  Pallas kernels: 27.2 us -> 29.9 us
  other arithmetic: 0.7 us -> 0 us
    unnamed x14 -> x0, local copies, waits for them, and re-layouts: 5.35 us -> none
    pallas_call x0 -> x1, Pallas kernels: none -> 1.93 us  [shards(): pl.pallas_call(store, out_shape=(jax.ShapeDtypeStruct((1,) + out.shape, B...]
    pallas_call x1, Pallas kernels: 27.2 us -> 28 us  [shards(): pl.pallas_call(functools.partial(kernel, n, heads), out_shape=(jax.ShapeD...]
    concatenate x1 -> x0, other arithmetic: 0.7 us -> none  [shards(): positions = jnp.concatenate([frame_index, row_index, column_index], axis=0)]
where the time goes in v2:
time: 31.4 us; the launch traced here: 31.2 us
  Pallas kernels  29.9 us (95%)
  between operations  1.29 us (4%)
    pallas_call x1, Pallas kernels, shards(): pl.pallas_call(functools.partial(kernel, n, heads), out_shape=(jax.ShapeD...  28 us
    pallas_call x1, Pallas kernels, shards(): pl.pallas_call(store, out_shape=(jax.ShapeDtypeStruct((1,) + out.shape, B...  1.93 us

profile of v2, /device:TPU:0, one launch (start us, length us, event | category | flops | bytes accessed | tf_op | source)
XLA Modules:
  0.0 31.2 jit_solution(13820068908162797407)
XLA Ops:
  1.3 28.0 %shard_map.113 = (bf16[16,3072]{1,0:T(8,128)(2,1)}, bf16[256,1024]{1,0:T(8,128)(2,1)}) custom-call(bf16[3,32,1024]{2,1,0:T(8,128)(2,1)} %bitcast.10, bf16[3,256,1024]{2,1,0:T(8,128)(2,1)} %bitcast.9, s32[1,32]{1,0:T(1,128)} %frame_hbm.1, s32[1,32]{1,0:T(1,128)} %row_hbm.1, s32[1,32]{1,0:T(1,128)} %column_hbm.1, s32[1]{0:T(128)S(6)} %copy.12.len_ref, ...), custom_call_target="tpu_custom_call" | custom-call | tf_op jit(solution)/shard_map/pallas_call | solution.py:296
  29.3 1.9 %shard_map.114 = (bf16[1,16,3072]{2,1,0:T(8,128)(2,1)}, bf16[1,256,1024]{2,1,0:T(8,128)(2,1)}) custom-call(bf16[16,3072]{1,0:T(8,128)(2,1)} %get-tuple-element.4.img_ref, bf16[256,1024]{1,0:T(8,128)(2,1)} %get-tuple-element.5.txt_ref), custom_call_target="tpu_custom_call" | custom-call | tf_op jit(solution)/shard_map/pallas_call | solution.py:337

commit v3 on v2

--- a/solution.py
+++ b/solution.py
@@ -25,9 +25,10 @@
 
 def kernel(
     n, heads, img_hbm, txt_hbm, frame_hbm, row_hbm, column_hbm, len_ref, res_hbm, w_hbm, bias_hbm, gate_hbm,
+    out_hbm, txt_out_hbm,
     out_ref, txt_out,
     img_ref, txt_q, places, q_send, k_send, q_all, k_all, v_all, a_send, home, t_send, w, res, bias, gate, p_send, p_recv,
-    local_sem, q_ss, q_rs, k_ss, k_rs, v_ss, v_rs, a_ss, a_rs, t1_ss, t2_ss, t_rs, p_ss, p_rs,
+    local_sem, q_ss, q_rs, k_ss, k_rs, kr_ss, v_ss, v_rs, vr_ss, a_ss, a_rs, t1_ss, t2_ss, t_rs, p_ss, p_rs,
 ):
     p = lax.axis_index("seq")
     t = lax.axis_index("tp")
@@ -124,15 +125,28 @@
             device_id={"seq": h * groups + group},
         )
 
-    def k_copy(d, s):
-        return pltpu.make_async_remote_copy(
-            k_send.at[d // groups], k_all.at[rows(s)], k_ss.at[d], k_rs.at[s], device_id={"seq": d}
-        )
-
-    def v_copy(d, s):
-        return pltpu.make_async_remote_copy(
-            img_ref.at[2, :, cols(d // groups)], v_all.at[rows(s)], v_ss.at[d], v_rs.at[s],
-            device_id={"seq": d},
+    def k_copy(h, s):
+        return pltpu.make_async_remote_copy(
+            k_send.at[h], k_all.at[rows(s)], k_ss.at[h], k_rs.at[s],
+            device_id={"seq": h * groups + group},
+        )
+
+    def v_copy(h, s):
+        return pltpu.make_async_remote_copy(
+            img_ref.at[2, :, cols(h)], v_all.at[rows(s)], v_ss.at[h], v_rs.at[s],
+            device_id={"seq": h * groups + group},
+        )
+
+    def k_relay(j, o, s):
+        return pltpu.make_async_remote_copy(
+            k_all.at[rows(s)], k_all.at[rows(s)], kr_ss.at[j, o], k_rs.at[s],
+            device_id={"seq": head * groups + (group + o) % groups},
+        )
+
+    def v_relay(j, o, s):
+        return pltpu.make_async_remote_copy(
+            v_all.at[rows(s)], v_all.at[rows(s)], vr_ss.at[j, o], v_rs.at[s],
+            device_id={"seq": head * groups + (group + o) % groups},
         )
 
     def a_copy(j, h):
@@ -148,13 +162,36 @@
 
         lax.fori_loop(1, count, step, 0)
 
-    over(n, lambda o: k_copy((p + o) % n, p).start())
+    over(heads, lambda o: k_copy((head + o) % heads, p).start())
+    k_all[rows(p), :] = k_send[head]
+    over(groups, lambda o: k_relay(head, o, p).start())
+    over(heads, lambda o: v_copy((head + o) % heads, p).start())
+    v_all[rows(p), :] = img_ref[2, :, cols(head)]
+    over(groups, lambda o: v_relay(head, o, p).start())
     over(heads, lambda o: q_copy((head + o) % heads, head).start())
-    over(n, lambda o: v_copy((p + o) % n, p).start())
-
     q_all[rows(head), :] = q_send[head]
-    k_all[rows(p), :] = k_send[head]
-    v_all[rows(p), :] = img_ref[2, :, cols(head)]
+
+    def pass_on(copy, relay):
+        def one(o):
+            j = (head + heads - o) % heads
+            s = j * groups + group
+            copy((head + o) % heads, s).wait_recv()
+            over(groups, lambda g: relay(j, g, s).start())
+
+        over(heads, one)
+
+    def arrive(relay):
+        def one(o):
+            def from_line(j, carry):
+                relay(j, o, j * groups + (group + o) % groups).wait_recv()
+                return carry
+
+            lax.fori_loop(0, heads, from_line, 0)
+
+        over(groups, one)
+
+    pass_on(k_copy, k_relay)
+    pass_on(v_copy, v_relay)
     for load in middle:
         load.wait()
     length = len_ref[0]
@@ -172,11 +209,11 @@
     def blend(weights, total):
         return jnp.dot(weights, v_all[...], preferred_element_type=F32) / total
 
-    over(n, lambda o: k_copy((p + o) % n, (p + n - o) % n).wait_recv())
+    arrive(k_relay)
     text_weights, text_total = weigh(txt_q[...])
     over(heads, lambda o: q_copy((head + o) % heads, (head + heads - o) % heads).wait_recv())
     image_weights, image_total = weigh(q_all[...])
-    over(n, lambda o: v_copy((p + o) % n, (p + n - o) % n).wait_recv())
+    arrive(v_relay)
     text_done = blend(text_weights, text_total)
     text_row = lax.broadcasted_iota(jnp.int32, text_done.shape, 0) + group * share
     text_done = jnp.where(text_row < length, text_done, 0.0).astype(BF16)
@@ -232,6 +269,21 @@
         p_copy(c).start()
         at = slice(c * width, (c + 1) * width)
         mine.append(jnp.where(t == 0, top, bottom))
+    def finish_plane(o):
+        def one(i, carry):
+            s = i * plane + (p % plane + o) % plane
+            plane_copy(None, o, s).wait_recv()
+            return carry
+
+        lax.fori_loop(0, lines, one, 0)
+        plane_copy(None, o, p).wait_send()
+
+    over(plane, finish_plane)
+    stores = [
+        pltpu.make_async_copy(src, dst, local_sem.at[11 + i])
+        for i, (src, dst) in enumerate(((txt_out, txt_out_hbm), (out_ref, out_hbm)))
+    ]
+    stores[0].start()
     for c in range(chunks):
         at = slice(c * width, (c + 1) * width)
         p_copy(c).wait_recv()
@@ -239,40 +291,51 @@
         out_ref[:, at] = (
             res[:, at].astype(F32) + gate[:, at] * (projected + bias[:, at])
         ).astype(BF16)
+    stores[1].start()
 
     def finish_line(i):
         s = (p + n - i * plane) % n
         over(plane, lambda o: plane_copy(i, o, s).wait_send())
         line_copy(i, s).wait_send()
 
-    def finish_plane(o):
-        def one(i, carry):
-            s = i * plane + (p % plane + o) % plane
-            plane_copy(None, o, s).wait_recv()
-            return carry
-
-        lax.fori_loop(0, lines, one, 0)
-        plane_copy(None, o, p).wait_send()
-
-    over(plane, finish_plane)
     over(lines, finish_line)
-    over(n, lambda o: k_copy((p + o) % n, p).wait_send())
-    over(n, lambda o: v_copy((p + o) % n, p).wait_send())
+    def finish_relay(relay):
+        def one(o):
+            def to_line(j, carry):
+                relay(j, o, j * groups + group).wait_send()
+                return carry
+
+            lax.fori_loop(0, heads, to_line, 0)
+
+        over(groups, one)
+
+    finish_relay(k_relay)
+    finish_relay(v_relay)
+    over(heads, lambda o: k_copy((head + o) % heads, p).wait_send())
+    over(heads, lambda o: v_copy((head + o) % heads, p).wait_send())
     over(heads, lambda o: q_copy((head + o) % heads, head).wait_send())
     over(heads, lambda o: a_copy((head + o) % heads, head).wait_send())
     for c in range(chunks):
         p_copy(c).wait_send()
-
-
-def store(img_ref, txt_ref, img_hbm, txt_hbm, sem):
-    copies = [
-        pltpu.make_async_copy(txt_ref, txt_hbm.at[0], sem.at[0]),
-        pltpu.make_async_copy(img_ref, img_hbm.at[0], sem.at[1]),
-    ]
-    for copy in copies:
-        copy.start()
-    for copy in copies:
+    for copy in stores:
         copy.wait()
+
+
+def store(img_in, txt_in, img_out, txt_out, img, txt, load_sem, store_sem):
+    pieces = load_sem.shape[0] - 1
+    rows = txt.shape[0] // pieces
+    parts = [(txt_in.at[pl.ds(i * rows, rows)], txt.at[pl.ds(i * rows, rows)],
+              txt_out.at[0, pl.ds(i * rows, rows)]) for i in range(pieces)]
+    parts.append((img_in, img, img_out.at[0]))
+    loads = [pltpu.make_async_copy(a, b, load_sem.at[i]) for i, (a, b, c) in enumerate(parts)]
+    stores = [pltpu.make_async_copy(b, c, store_sem.at[i]) for i, (a, b, c) in enumerate(parts)]
+    for load in loads:
+        load.start()
+    for load, put in zip(loads, stores):
+        load.wait()
+        put.start()
+    for put in stores:
+        put.wait()
 
 
 def shards(img_qkv, txt_qkv, frame_index, row_index, column_index, txt_len, residual, w_proj, proj_bias, gate):
@@ -290,7 +353,6 @@
     chunks = 4
     img = img_qkv[0].transpose(1, 0, 2)
     txt = txt_qkv[0].transpose(1, 0, 2)
-    vmem = pl.BlockSpec(memory_space=pltpu.VMEM)
     hbm = pl.BlockSpec(memory_space=pltpu.HBM)
     dma = pltpu.SemaphoreType.DMA
     out, txt_out = pl.pallas_call(
@@ -300,8 +362,10 @@
             jax.ShapeDtypeStruct((text, channels), BF16),
         ),
         in_specs=[hbm] * 5 + [pl.BlockSpec(memory_space=pltpu.SMEM)] + [hbm] * 4,
-        out_specs=(vmem, vmem),
+        out_specs=(hbm, hbm),
         scratch_shapes=[
+            pltpu.VMEM((half, model), BF16),
+            pltpu.VMEM((text, channels), BF16),
             pltpu.VMEM((3, tokens, channels), BF16),
             pltpu.VMEM((share, HD), BF16),
             pltpu.VMEM((3, 1, tokens), jnp.int32),
@@ -319,10 +383,10 @@
             pltpu.VMEM((1, model), F32),
             pltpu.VMEM((chunks, half, model // chunks), BF16),
             pltpu.VMEM((chunks, half, model // chunks), BF16),
-            dma((11,)),
+            dma((13,)),
             dma((heads,)), dma((heads,)),
-            dma((n,)), dma((n,)),
-            dma((n,)), dma((n,)),
+            dma((heads,)), dma((n,)), dma((heads, groups)),
+            dma((heads,)), dma((n,)), dma((heads, groups)),
             dma((heads,)), dma((heads,)),
             dma((lines,)), dma((lines, plane)), dma((n,)),
             dma((chunks,)), dma((chunks,)),
@@ -340,9 +404,11 @@
             jax.ShapeDtypeStruct((1,) + out.shape, BF16),
             jax.ShapeDtypeStruct((1,) + txt_out.shape, BF16),
         ),
-        in_specs=[vmem, vmem],
+        in_specs=[hbm, hbm],
         out_specs=(hbm, hbm),
-        scratch_shapes=[dma((2,))],
+        scratch_shapes=[
+            pltpu.VMEM(out.shape, BF16), pltpu.VMEM(txt_out.shape, BF16), dma((5,)), dma((5,)),
+        ],
         compiler_params=pltpu.CompilerParams(vmem_limit_bytes=66400000),
     )(out, txt_out)
 

time: 31.4 us -> 30.1 us (0.959)
  Pallas kernels: 29.9 us -> 28.6 us
    pallas_call x1, Pallas kernels: 28 us -> 26.8 us  [shards(): pl.pallas_call(functools.partial(kernel, n, heads), out_shape=(jax.ShapeD...]
where the time goes in v3:
time: 30.1 us; the launch traced here: 29.9 us
  Pallas kernels  28.6 us (95%)
  between operations  1.29 us (4%)
    pallas_call x1, Pallas kernels, shards(): pl.pallas_call(functools.partial(kernel, n, heads), out_shape=(jax.ShapeD...  26.8 us
    pallas_call x1, Pallas kernels, shards(): pl.pallas_call(store, out_shape=(jax.ShapeDtypeStruct((1,) + out.shape, B...  1.88 us

profile of v3, /device:TPU:0, one launch (start us, length us, event | category | flops | bytes accessed | tf_op | source)
XLA Modules:
  0.0 29.9 jit_solution(9785776501979019351)
XLA Ops:
  1.3 26.8 %shard_map.113 = (bf16[16,3072]{1,0:T(8,128)(2,1)}, bf16[256,1024]{1,0:T(8,128)(2,1)}) custom-call(bf16[3,32,1024]{2,1,0:T(8,128)(2,1)} %bitcast.10, bf16[3,256,1024]{2,1,0:T(8,128)(2,1)} %bitcast.9, s32[1,32]{1,0:T(1,128)} %frame_hbm.1, s32[1,32]{1,0:T(1,128)} %row_hbm.1, s32[1,32]{1,0:T(1,128)} %column_hbm.1, s32[1]{0:T(128)S(6)} %copy.12.len_ref, ...), custom_call_target="tpu_custom_call" | custom-call | tf_op jit(solution)/shard_map/pallas_call | solution.py:358
  28.0 1.9 %shard_map.114 = (bf16[1,16,3072]{2,1,0:T(8,128)(2,1)}, bf16[1,256,1024]{2,1,0:T(8,128)(2,1)}) custom-call(bf16[16,3072]{1,0:T(8,128)(2,1)} %get-tuple-element.4.img_in, bf16[256,1024]{1,0:T(8,128)(2,1)} %get-tuple-element.5.txt_in), custom_call_target="tpu_custom_call" | custom-call | tf_op jit(solution)/shard_map/pallas_call | solution.py:401

commit v4 on v3

--- a/solution.py
+++ b/solution.py
@@ -319,23 +319,6 @@
         p_copy(c).wait_send()
     for copy in stores:
         copy.wait()
-
-
-def store(img_in, txt_in, img_out, txt_out, img, txt, load_sem, store_sem):
-    pieces = load_sem.shape[0] - 1
-    rows = txt.shape[0] // pieces
-    parts = [(txt_in.at[pl.ds(i * rows, rows)], txt.at[pl.ds(i * rows, rows)],
-              txt_out.at[0, pl.ds(i * rows, rows)]) for i in range(pieces)]
-    parts.append((img_in, img, img_out.at[0]))
-    loads = [pltpu.make_async_copy(a, b, load_sem.at[i]) for i, (a, b, c) in enumerate(parts)]
-    stores = [pltpu.make_async_copy(b, c, store_sem.at[i]) for i, (a, b, c) in enumerate(parts)]
-    for load in loads:
-        load.start()
-    for load, put in zip(loads, stores):
-        load.wait()
-        put.start()
-    for put in stores:
-        put.wait()
 
 
 def shards(img_qkv, txt_qkv, frame_index, row_index, column_index, txt_len, residual, w_proj, proj_bias, gate):
@@ -398,19 +381,7 @@
         img, txt, frame_index, row_index, column_index, txt_len, residual[0], w_proj,
         proj_bias[None], gate[None],
     )
-    return pl.pallas_call(
-        store,
-        out_shape=(
-            jax.ShapeDtypeStruct((1,) + out.shape, BF16),
-            jax.ShapeDtypeStruct((1,) + txt_out.shape, BF16),
-        ),
-        in_specs=[hbm, hbm],
-        out_specs=(hbm, hbm),
-        scratch_shapes=[
-            pltpu.VMEM(out.shape, BF16), pltpu.VMEM(txt_out.shape, BF16), dma((5,)), dma((5,)),
-        ],
-        compiler_params=pltpu.CompilerParams(vmem_limit_bytes=66400000),
-    )(out, txt_out)
+    return out[None], txt_out[None]
 
 
 def solution(mesh):

time: 30.1 us -> 31.7 us (1.053)
  local copies, waits for them, and re-layouts: 0 us -> 3.41 us
  Pallas kernels: 28.6 us -> 26.8 us
    unnamed x0 -> x2, local copies, waits for them, and re-layouts: none -> 3.41 us
    pallas_call x1 -> x0, Pallas kernels: 1.88 us -> none  [shards(): pl.pallas_call(store, out_shape=(jax.ShapeDtypeStruct((1,) + out.shape, B...]
where the time goes in v4:
time: 31.7 us; the launch traced here: 31.5 us
  Pallas kernels  26.8 us (85%)
  local copies, waits for them, and re-layouts  3.41 us (11%)
  between operations  1.29 us (4%)
    pallas_call x1, Pallas kernels, shards(): pl.pallas_call(functools.partial(kernel, n, heads), out_shape=(jax.ShapeD...  26.8 us
    unnamed x2, local copies, waits for them, and re-layouts  3.41 us

profile of v4, /device:TPU:0, one launch (start us, length us, event | category | flops | bytes accessed | tf_op | source)
XLA Modules:
  0.0 31.5 jit_solution(5080269798481097707)
XLA Ops:
  1.3 26.8 %shard_map.113 = (bf16[16,3072]{1,0:T(8,128)(2,1)}, bf16[256,1024]{1,0:T(8,128)(2,1)}) custom-call(bf16[3,32,1024]{2,1,0:T(8,128)(2,1)} %bitcast.13, bf16[3,256,1024]{2,1,0:T(8,128)(2,1)} %bitcast.11, s32[1,32]{1,0:T(1,128)} %frame_hbm.1, s32[1,32]{1,0:T(1,128)} %row_hbm.1, s32[1,32]{1,0:T(1,128)} %column_hbm.1, s32[1]{0:T(128)S(6)} %copy.14.len_ref, ...), custom_call_target="tpu_custom_call" | custom-call | tf_op jit(solution)/shard_map/pallas_call | solution.py:341
  28.0 1.5 %copy.15 = bf16[1,16,3072]{2,1,0:T(8,128)(2,1)} copy(bf16[1,16,3072]{2,1,0:T(8,128)(2,1)} %bitcast.15) | data formatting | bytes 196608
  29.6 1.9 %copy.16 = bf16[1,256,1024]{2,1,0:T(8,128)(2,1)} copy(bf16[1,256,1024]{2,1,0:T(8,128)(2,1)} %bitcast.12) | data formatting | bytes 1048576
